TPU v7x, 32 devices: a whole 2x2x4 slice. The times are simulated.
32 devices in a mesh: rows: 8 (over z, core), aux: 4 (over y, x).
Axes of the slice: x: 2, y: 2, z: 4, core: 2. Of those that a mesh axis runs over, the one named last changes fastest.
Arguments:
- pair_coeffs: float32 [36000, 8192], P('aux', 'rows'), may hold values from -0.0625 to 0.0625
- pair_gaps: float32 [8192], P('rows'), may hold values from 0.2 to 20
- trial_vectors: float32 [36000, 128], P('aux'), may hold values from -0.03125 to 0.03125
Outputs:
- vectors_out: float32 [36000, 128], P('aux')
- rayleigh: float32 [128, 128], replicated
All inputs are finite; a program needn't handle non-finite values.
Results may differ from a plain program's by a relative error of at most 0.00011.
Values sent between devices are 32-bit elements; how exact they have to be, the bound alone decides.
A program may use at most 128 MiB of HBM per device.

v0:
```python
import jax
import jax.numpy as jnp
from jax import lax
from jax.sharding import PartitionSpec as P

ITERS = 2


def project(coeffs, vectors_now):
    return lax.dot_general(
        coeffs,
        vectors_now,
        (((0,), (0,)), ((), ())),
        precision=lax.Precision.HIGHEST,
        preferred_element_type=jnp.float32,
    )


def shards(pair_coeffs, pair_gaps, trial_vectors):
    highest = lax.Precision.HIGHEST
    weights = 4.0 * pair_gaps / (pair_gaps * pair_gaps + 1.0)

    def forward(vectors_now):
        projected = lax.psum(project(pair_coeffs, vectors_now), "aux")
        return (projected, weights)

    vectors_now = trial_vectors
    for step in range(ITERS):
        apply_projected, apply_row_weights = forward(vectors_now)
        scaled = apply_row_weights[:, None] * apply_projected
        partial_sum = jnp.dot(
            pair_coeffs, scaled, precision=highest, preferred_element_type=jnp.float32
        )
        applied = lax.psum(partial_sum, "rows")
        local_gram = jnp.dot(
            applied.T, applied, precision=highest, preferred_element_type=jnp.float32
        )
        correlation = lax.psum(local_gram, "aux")
        factor = jnp.linalg.cholesky(correlation)
        vectors_now = jax.scipy.linalg.solve_triangular(factor, applied.T, lower=True).T
    final_proj, row_weights = forward(vectors_now)
    local_rayleigh = jnp.dot(
        final_proj.T,
        row_weights[:, None] * final_proj,
        precision=highest,
        preferred_element_type=jnp.float32,
    )
    rayleigh = lax.psum(local_rayleigh, "rows")
    return (vectors_now, rayleigh)


def solution(mesh):
    in_specs = (P("aux", "rows"), P("rows"), P("aux", None))
    out_specs = (P("aux", None), P())
    return jax.shard_map(shards, mesh=mesh, in_specs=in_specs, out_specs=out_specs, check_vma=False)
```

profile of v0, /device:TPU:0, one launch (start us, length us, event | category | flops | bytes accessed | tf_op | source)
XLA Modules:
  0.0 741.6 jit_solution(11998312503589431034)
XLA Ops:
  7.2 27.7 %fusion.19 = f32[1024,128]{0,1:T(8,128)} fusion(f32[9000,1024]{1,0:T(8,128)} %param.6, f32[9000,128]{1,0:T(8,128)} %param.8), kind=kOutput, calls=%fused_computation.33 | convolution fusion | flops 14155776000 | bytes 41996288 | tf_op jit(solution)/shard_map/dot_general | solution.py:10
  35.0 48.2 %all-reduce.9.cloned.1.call-done = f32[1024,128]{0,1:T(8,128)} async-done(((f32[1024,128]{0,1:T(8,128)}), f32[1024,128]{0,1:T(8,128)}) %all-reduce.9.cloned.1.call-update) | async-done | bytes 524304 | tf_op jit(solution)/shard_map/psum | solution.py:24
  83.2 33.3 %convolution_bitcast_fusion.1 = f32[9000,128]{1,0:T(8,128)} fusion(f32[9000,1024]{1,0:T(8,128)} %param.6, f32[1024,128]{0,1:T(8,128)} %all-reduce.9.cloned.1.call-done, f32[1024]{0:T(1024)S(1)} %add_divide_fusion), kind=kOutput, calls=%fused_computation.1 | convolution fusion | flops 14155907072 | bytes 42000384 | tf_op jit(solution)/shard_map/dot_general | solution.py:31
  116.8 104.8 %all-reduce.11.cloned.1.call-done = f32[9000,128]{1,0:T(8,128)} async-done(((f32[9000,128]{1,0:T(8,128)}), f32[9000,128]{1,0:T(8,128)}) %all-reduce.11.cloned.1.call-update) | async-done | bytes 4608016 | tf_op jit(solution)/shard_map/psum | solution.py:34
  221.5 11.8 %fusion.20 = f32[128,128]{0,1:T(8,128)} fusion(f32[9000,128]{1,0:T(8,128)} %all-reduce.11.cloned.1.call-done), kind=kOutput, calls=%fused_computation.34 | convolution fusion | flops 1769472000 | bytes 4673536 | tf_op jit(solution)/shard_map/dot_general | solution.py:35
  233.8 41.4 %all-reduce.13.cloned.1.call-done = f32[128,128]{0,1:T(8,128)} async-done(((f32[128,128]{0,1:T(8,128)}), f32[128,128]{0,1:T(8,128)}) %all-reduce.13.cloned.1.call-update) | async-done | bytes 65552 | tf_op jit(solution)/shard_map/psum | solution.py:38
  275.1 0.9 copy.6
  276.1 0.9 fusion.16
  276.9 11.7 %cholesky.44 = f32[128,128]{1,0:T(8,128)S(1)} custom-call(f32[128,128]{1,0:T(8,128)S(1)} %fusion.16), custom_call_target="Cholesky" | custom-call | tf_op jit(solution)/shard_map/jit(cholesky)/cholesky | solution.py:39
  288.7 0.6 compare_reduce_fusion.1
  289.3 0.7 fusion.11
  290.0 9.8 %custom-call.6 = f32[1,128,128]{1,2,0:T(8,128)S(1)} custom-call(f32[1,128,128]{2,1,0:T(8,128)S(1)} %fusion.11), custom_call_target="InvertDiagBlocksLowerTriangular" | custom-call | tf_op jit(solution)/shard_map/jit(_solve_triangular)/triangular_solve | solution.py:40
  299.8 6.1 fusion.2
  305.9 24.9 %convolution_bitcast_fusion.2 = f32[1024,128]{0,1:T(8,128)} fusion(f32[128,9000]{1,0:T(8,128)S(1)} %fusion.2, f32[9000,1024]{1,0:T(8,128)} %param.6), kind=kOutput, calls=%fused_computation.6 | convolution fusion | flops 14155776000 | bytes 41996288 | tf_op jit(solution)/shard_map/dot_general | solution.py:10
  331.1 45.3 %all-reduce.15.cloned.1.call-done = f32[1024,128]{0,1:T(8,128)} async-done(((f32[1024,128]{0,1:T(8,128)}), f32[1024,128]{0,1:T(8,128)}) %all-reduce.15.cloned.1.call-update) | async-done | bytes 524304 | tf_op jit(solution)/shard_map/psum | solution.py:24
  376.4 33.3 %convolution_bitcast_fusion = f32[9000,128]{1,0:T(8,128)} fusion(f32[9000,1024]{1,0:T(8,128)} %param.6, f32[1024,128]{0,1:T(8,128)} %all-reduce.15.cloned.1.call-done, f32[1024]{0:T(1024)S(1)} %add_divide_fusion), kind=kOutput, calls=%fused_computation | convolution fusion | flops 14155907072 | bytes 42000384 | tf_op jit(solution)/shard_map/dot_general | solution.py:31
  409.7 105.0 %all-reduce.17.cloned.1.call-done = f32[9000,128]{1,0:T(8,128)} async-done(((f32[9000,128]{1,0:T(8,128)}), f32[9000,128]{1,0:T(8,128)}) %all-reduce.17.cloned.1.call-update) | async-done | bytes 4608016 | tf_op jit(solution)/shard_map/psum | solution.py:34
  514.7 11.8 %fusion.21 = f32[128,128]{0,1:T(8,128)} fusion(f32[9000,128]{1,0:T(8,128)} %all-reduce.17.cloned.1.call-done), kind=kOutput, calls=%fused_computation.35 | convolution fusion | flops 1769472000 | bytes 4673536 | tf_op jit(solution)/shard_map/dot_general | solution.py:35
  526.7 41.5 %all-reduce.19.cloned.1.call-done = f32[128,128]{0,1:T(8,128)} async-done(((f32[128,128]{0,1:T(8,128)}), f32[128,128]{0,1:T(8,128)}) %all-reduce.19.cloned.1.call-update) | async-done | bytes 65552 | tf_op jit(solution)/shard_map/psum | solution.py:38
  568.3 0.9 copy.8
  569.2 0.9 fusion.14
  570.1 11.7 %cholesky.55 = f32[128,128]{1,0:T(8,128)S(1)} custom-call(f32[128,128]{1,0:T(8,128)S(1)} %fusion.14), custom_call_target="Cholesky" | custom-call | tf_op jit(solution)/shard_map/jit(cholesky)/cholesky | solution.py:39
  581.8 0.6 compare_reduce_fusion
  582.5 0.7 fusion.12
  583.1 9.8 %custom-call.7 = f32[1,128,128]{1,2,0:T(8,128)S(1)} custom-call(f32[1,128,128]{2,1,0:T(8,128)S(1)} %fusion.12), custom_call_target="InvertDiagBlocksLowerTriangular" | custom-call | tf_op jit(solution)/shard_map/jit(_solve_triangular)/triangular_solve | solution.py:40
  593.0 9.2 %fusion = f32[128,9000]{0,1:T(8,128)S(1)} fusion(f32[9000,128]{1,0:T(8,128)} %all-reduce.17.cloned.1.call-done, f32[1,128,128]{1,2,0:T(8,128)S(1)} %custom-call.7), kind=kOutput, calls=%fused_computation.2 | convolution fusion | flops 1769472000 | bytes 9281536 | tf_op jit(solution)/shard_map/jit(_solve_triangular)/triangular_solve | solution.py:40
  602.2 2.1 copy-done
  604.3 25.4 %convolution_bitcast_fusion.3 = f32[1024,128]{0,1:T(8,128)} fusion(f32[128,9000]{0,1:T(8,128)S(1)} %fusion, f32[9000,1024]{1,0:T(8,128)} %param.6), kind=kOutput, calls=%fused_computation.7 | convolution fusion | flops 14155776000 | bytes 41996288 | tf_op jit(solution)/shard_map/dot_general | solution.py:10
  629.8 45.5 %all-reduce.21.cloned.1.call-done = f32[1024,128]{0,1:T(8,128)} async-done(((f32[1024,128]{0,1:T(8,128)}), f32[1024,128]{0,1:T(8,128)}) %all-reduce.21.cloned.1.call-update) | async-done | bytes 524304 | tf_op jit(solution)/shard_map/psum | solution.py:24
  675.3 2.4 fusion.4
  677.7 55.2 %all-reduce.23.cloned.1.call-done = f32[128,128]{1,0:T(8,128)} async-done(((f32[128,128]{1,0:T(8,128)}), f32[128,128]{1,0:T(8,128)}) %all-reduce.23.cloned.1.call-update) | async-done | bytes 65552 | tf_op jit(solution)/shard_map/psum | solution.py:48
  732.9 1.5 copy.19
  (22 shorter events, 1.6 us)
Async XLA Ops:
  7.2 27.8 %copy-start.1 = (f32[1024]{0:T(1024)S(1)}, f32[1024]{0:T(1024)}, u32[]{:S(2)}) copy-start(f32[1024]{0:T(1024)} %param.7) | copy-start | bytes 12292
  7.2 76.0 %all-reduce.9.cloned.1.call-start = ((), (), s32[]{:S(2)}) async-start(), calls=%async_computation | async-start | bytes 1048576 | tf_op jit(solution)/shard_map/psum | solution.py:24
  34.9 186.6 %all-reduce.11.cloned.1.call-start = ((), (), s32[]{:S(2)}) async-start(), calls=%async_computation.1 | async-start | bytes 9216000 | tf_op jit(solution)/shard_map/psum | solution.py:34
  116.5 158.6 %all-reduce.13.cloned.1.call-start = ((), (), s32[]{:S(2)}) async-start(), calls=%async_computation.2 | async-start | bytes 131072 | tf_op jit(solution)/shard_map/psum | solution.py:38
  233.3 143.0 %all-reduce.15.cloned.1.call-start = ((), (), s32[]{:S(2)}) async-start(), calls=%async_computation.3 | async-start | bytes 1048576 | tf_op jit(solution)/shard_map/psum | solution.py:24
  330.8 183.9 %all-reduce.17.cloned.1.call-start = ((), (), s32[]{:S(2)}) async-start(), calls=%async_computation.4 | async-start | bytes 9216000 | tf_op jit(solution)/shard_map/psum | solution.py:34
  409.7 158.6 %all-reduce.19.cloned.1.call-start = ((), (), s32[]{:S(2)}) async-start(), calls=%async_computation.5 | async-start | bytes 131072 | tf_op jit(solution)/shard_map/psum | solution.py:38
  526.5 148.8 %all-reduce.21.cloned.1.call-start = ((), (), s32[]{:S(2)}) async-start(), calls=%async_computation.6 | async-start | bytes 1048576 | tf_op jit(solution)/shard_map/psum | solution.py:24
  602.2 2.2 copy-start
  629.8 103.1 %all-reduce.23.cloned.1.call-start = ((), (), s32[]{:S(2)}) async-start(), calls=%async_computation.7 | async-start | bytes 131072 | tf_op jit(solution)/shard_map/psum | solution.py:48
Sparse Core Ops, SparseCore 0:
  35.1 48.0 all-reduce.8
  116.6 104.8 all-reduce.10
  233.5 41.6 all-reduce.12
  331.0 45.3 all-reduce.14
  409.8 104.8 all-reduce.16
  526.6 41.6 all-reduce.18
  629.9 45.3 all-reduce.20
  678.2 54.6 all-reduce.22
where the time goes:
time: 748 us; the launch traced here: 742 us
  waiting for transfers between devices  487 us (65%)
  matrix products  186 us (25%)
  other arithmetic  47.4 us (6%)
  between operations  14.6 us (2%)
    psum x2, waiting for transfers between devices, shards(): applied = lax.psum(partial_sum, 'rows')  210 us
    psum x3, waiting for transfers between devices, forward(): projected = lax.psum(project(pair_coeffs, vectors_now), 'aux')  139 us
    psum x2, waiting for transfers between devices, shards(): correlation = lax.psum(local_gram, 'aux')  82.9 us
    dot_general x3, matrix products, project(): lax.dot_general(coeffs, vectors_now, (((0,), (0,)), ((), ())), precision=...  78 us
    dot_general x2, matrix products, shards(): jnp.dot(pair_coeffs, scaled, precision=highest, preferred_element_type=jn...  66.6 us
    psum x1, waiting for transfers between devices, shards(): rayleigh = lax.psum(local_rayleigh, 'rows')  55.2 us
    another operation x6, other arithmetic, shards(): factor = jnp.linalg.cholesky(correlation)  24.8 us
    dot_general x2, matrix products, shards(): jnp.dot(applied.T, applied, precision=highest, preferred_element_type=jnp...  23.5 us
  transfers between devices with their start and end apart: 8, of which 8 were waited for; matrix products, arithmetic and copies ran while one was open for 0% of the time, Pallas kernels for 0%

commit v1 on v0

--- a/solution.py
+++ b/solution.py
@@ -31,7 +31,11 @@
         partial_sum = jnp.dot(
             pair_coeffs, scaled, precision=highest, preferred_element_type=jnp.float32
         )
-        applied = lax.psum(partial_sum, "rows")
+        applied = partial_sum
+        for hop in (1, 2, 4):
+            applied = applied + lax.ppermute(
+                applied, "rows", [(dev, dev ^ hop) for dev in range(8)]
+            )
         local_gram = jnp.dot(
             applied.T, applied, precision=highest, preferred_element_type=jnp.float32
         )

time: 748 us -> 1160 us (1.55)
  waiting for transfers between devices: 487 us -> 888 us
    ppermute x0 -> x6, waiting for transfers between devices: none -> 611 us  [shards(): lax.ppermute(applied, 'rows', [(dev, dev ^ hop) for dev in range(8)])]
    psum x2 -> x0, waiting for transfers between devices: 210 us -> none  [shards(): applied = lax.psum(partial_sum, 'rows')]
  transfers between devices with their start and end apart: 8 -> 12, of which waited for: 8 -> 12; matrix products, arithmetic and copies ran while one was open for 0% -> 0% of each run, Pallas kernels for 0% -> 0%
where the time goes in v1:
time: 1160 us
  waiting for transfers between devices  888 us (77%)
  matrix products  184 us (16%)
  other arithmetic  50.2 us (4%)
  between operations  14.8 us (1%)
    ppermute x6, waiting for transfers between devices, shards(): lax.ppermute(applied, 'rows', [(dev, dev ^ hop) for dev in range(8)])  611 us
    psum x3, waiting for transfers between devices, forward(): projected = lax.psum(project(pair_coeffs, vectors_now), 'aux')  139 us
    psum x2, waiting for transfers between devices, shards(): correlation = lax.psum(local_gram, 'aux')  83.2 us
    dot_general x3, matrix products, project(): lax.dot_general(coeffs, vectors_now, (((0,), (0,)), ((), ())), precision=...  78 us
    dot_general x2, matrix products, shards(): jnp.dot(pair_coeffs, scaled, precision=highest, preferred_element_type=jn...  68.9 us
    psum x1, waiting for transfers between devices, shards(): rayleigh = lax.psum(local_rayleigh, 'rows')  55 us
    another operation x6, other arithmetic, shards(): factor = jnp.linalg.cholesky(correlation)  24.8 us
  transfers between devices with their start and end apart: 12, of which 12 were waited for; matrix products, arithmetic and copies ran while one was open for 0% of the time, Pallas kernels for 0%

profile of v1, /device:TPU:0, one launch (start us, length us, event | category | flops | bytes accessed | tf_op | source)
XLA Modules:
  0.0 1156.1 jit_solution(14519239360382614564)
XLA Ops:
  7.2 27.7 %fusion.25 = f32[1024,128]{0,1:T(8,128)} fusion(f32[9000,1024]{1,0:T(8,128)} %param.6, f32[9000,128]{1,0:T(8,128)} %param.8), kind=kOutput, calls=%fused_computation.39 | convolution fusion | flops 14155776000 | bytes 41996288 | tf_op jit(solution)/shard_map/dot_general | solution.py:10
  35.0 48.2 %all-reduce.7.cloned.1.call-done = f32[1024,128]{0,1:T(8,128)} async-done(((f32[1024,128]{0,1:T(8,128)}), f32[1024,128]{0,1:T(8,128)}) %all-reduce.7.cloned.1.call-update) | async-done | bytes 524304 | tf_op jit(solution)/shard_map/psum | solution.py:24
  83.2 34.4 %convolution_bitcast_fusion.1 = f32[9000,128]{1,0:T(8,128)S(1)} fusion(f32[9000,1024]{1,0:T(8,128)} %param.6, f32[1024,128]{0,1:T(8,128)} %all-reduce.7.cloned.1.call-done, f32[1024]{0:T(1024)S(1)} %add_divide_fusion), kind=kOutput, calls=%fused_computation.1 | convolution fusion | flops 14155907072 | bytes 42000384 | tf_op jit(solution)/shard_map/dot_general | solution.py:31
  117.7 7.7 collective-permute-done
  127.5 100.0 %collective-permute-done.1 = f32[9000,128]{1,0:T(8,128)S(1)} collective-permute-done((f32[9000,128]{1,0:T(8,128)S(1)}, f32[9000,128]{1,0:T(8,128)S(1)}, u32[]{:S(2)}, u32[]{:S(2)}) %collective-permute-start.1) | collective-permute-done | bytes 4608032 | tf_op jit(solution)/shard_map/ppermute | solution.py:36
  228.4 2.5 collective-permute-start.2
  230.9 197.9 %collective-permute-done.2 = f32[9000,128]{1,0:T(8,128)S(1)} collective-permute-done((f32[9000,128]{1,0:T(8,128)S(1)}, f32[9000,128]{1,0:T(8,128)S(1)}, u32[]{:S(2)}, u32[]{:S(2)}) %collective-permute-start.2) | collective-permute-done | bytes 4608032 | tf_op jit(solution)/shard_map/ppermute | solution.py:36
  428.8 2.1 copy-done.3
  430.8 8.7 fusion.8
  440.0 41.5 %all-reduce.9.cloned.1.call-done = f32[128,128]{0,1:T(8,128)} async-done(((f32[128,128]{0,1:T(8,128)}), f32[128,128]{0,1:T(8,128)}) %all-reduce.9.cloned.1.call-update) | async-done | bytes 65552 | tf_op jit(solution)/shard_map/psum | solution.py:42
  483.3 11.7 %cholesky.44 = f32[128,128]{1,0:T(8,128)S(1)} custom-call(f32[128,128]{1,0:T(8,128)S(1)} %fusion.22), custom_call_target="Cholesky" | custom-call | tf_op jit(solution)/shard_map/jit(cholesky)/cholesky | solution.py:43
  496.4 9.8 custom-call.6
  506.2 7.0 fusion.2
  513.1 24.9 %convolution_bitcast_fusion.2 = f32[1024,128]{0,1:T(8,128)} fusion(f32[128,9000]{1,0:T(8,128)S(1)} %fusion.2, f32[9000,1024]{1,0:T(8,128)} %param.6), kind=kOutput, calls=%fused_computation.12 | convolution fusion | flops 14155776000 | bytes 41996288 | tf_op jit(solution)/shard_map/dot_general | solution.py:10
  538.3 45.3 %all-reduce.11.cloned.1.call-done = f32[1024,128]{0,1:T(8,128)} async-done(((f32[1024,128]{0,1:T(8,128)}), f32[1024,128]{0,1:T(8,128)}) %all-reduce.11.cloned.1.call-update) | async-done | bytes 524304 | tf_op jit(solution)/shard_map/psum | solution.py:24
  583.6 34.4 %convolution_bitcast_fusion = f32[9000,128]{1,0:T(8,128)S(1)} fusion(f32[9000,1024]{1,0:T(8,128)} %param.6, f32[1024,128]{0,1:T(8,128)} %all-reduce.11.cloned.1.call-done, f32[1024]{0:T(1024)S(1)} %add_divide_fusion), kind=kOutput, calls=%fused_computation | convolution fusion | flops 14155907072 | bytes 42000384 | tf_op jit(solution)/shard_map/dot_general | solution.py:31
  618.1 7.7 collective-permute-done.3
  626.3 1.6 collective-permute-start.4
  627.9 100.0 %collective-permute-done.4 = f32[9000,128]{1,0:T(8,128)S(1)} collective-permute-done((f32[9000,128]{1,0:T(8,128)S(1)}, f32[9000,128]{1,0:T(8,128)S(1)}, u32[]{:S(2)}, u32[]{:S(2)}) %collective-permute-start.4) | collective-permute-done | bytes 4608032 | tf_op jit(solution)/shard_map/ppermute | solution.py:36
  728.8 2.5 collective-permute-start.5
  731.3 197.9 %collective-permute-done.5 = f32[9000,128]{1,0:T(8,128)S(1)} collective-permute-done((f32[9000,128]{1,0:T(8,128)S(1)}, f32[9000,128]{1,0:T(8,128)S(1)}, u32[]{:S(2)}, u32[]{:S(2)}) %collective-permute-start.5) | collective-permute-done | bytes 4608032 | tf_op jit(solution)/shard_map/ppermute | solution.py:36
  929.1 2.1 copy-done.4
  931.2 8.7 fusion.5
  940.2 41.7 %all-reduce.13.cloned.1.call-done = f32[128,128]{0,1:T(8,128)} async-done(((f32[128,128]{0,1:T(8,128)}), f32[128,128]{0,1:T(8,128)}) %all-reduce.13.cloned.1.call-update) | async-done | bytes 65552 | tf_op jit(solution)/shard_map/psum | solution.py:42
  983.7 11.7 %cholesky.55 = f32[128,128]{1,0:T(8,128)S(1)} custom-call(f32[128,128]{1,0:T(8,128)S(1)} %fusion.20), custom_call_target="Cholesky" | custom-call | tf_op jit(solution)/shard_map/jit(cholesky)/cholesky | solution.py:43
  996.7 9.8 custom-call.7
  1006.5 10.2 fusion
  1016.8 2.1 copy-done.2
  1018.9 25.4 %convolution_bitcast_fusion.3 = f32[1024,128]{0,1:T(8,128)} fusion(f32[128,9000]{0,1:T(8,128)S(1)} %fusion, f32[9000,1024]{1,0:T(8,128)} %param.6), kind=kOutput, calls=%fused_computation.13 | convolution fusion | flops 14155776000 | bytes 41996288 | tf_op jit(solution)/shard_map/dot_general | solution.py:10
  1044.4 45.5 %all-reduce.15.cloned.1.call-done = f32[1024,128]{0,1:T(8,128)} async-done(((f32[1024,128]{0,1:T(8,128)}), f32[1024,128]{0,1:T(8,128)}) %all-reduce.15.cloned.1.call-update) | async-done | bytes 524304 | tf_op jit(solution)/shard_map/psum | solution.py:24
  1089.8 2.4 fusion.10
  1092.3 55.0 %all-reduce.17.cloned.1.call-done = f32[128,128]{1,0:T(8,128)} async-done(((f32[128,128]{1,0:T(8,128)}), f32[128,128]{1,0:T(8,128)}) %all-reduce.17.cloned.1.call-update) | async-done | bytes 65552 | tf_op jit(solution)/shard_map/psum | solution.py:52
  (40 shorter events, 13.4 us)
Async XLA Ops:
  7.2 27.8 %copy-start.5 = (f32[1024]{0:T(1024)S(1)}, f32[1024]{0:T(1024)}, u32[]{:S(2)}) copy-start(f32[1024]{0:T(1024)} %param.7) | copy-start | bytes 12292
  7.2 76.0 %all-reduce.7.cloned.1.call-start = ((), (), s32[]{:S(2)}) async-start(), calls=%async_computation | async-start | bytes 1048576 | tf_op jit(solution)/shard_map/psum | solution.py:24
  34.9 446.6 %all-reduce.9.cloned.1.call-start = ((), (), s32[]{:S(2)}) async-start(), calls=%async_computation.1 | async-start | bytes 131072 | tf_op jit(solution)/shard_map/psum | solution.py:42
  117.6 7.8 collective-permute-start
  126.0 101.5 %collective-permute-start.1 = (f32[9000,128]{1,0:T(8,128)S(1)}, f32[9000,128]{1,0:T(8,128)S(1)}, u32[]{:S(2)}, u32[]{:S(2)}) collective-permute-start(f32[9000,128]{1,0:T(8,128)S(1)} %add.47), channel_id=1, source_target_pairs={{0,8},{4,12},{8,0},{12,4},{16,24},{20,28},{24,16},{28,20},{1,9},{5... | collective-permute-start | bytes 13824008 | tf_op jit(solution)/shard_map/ppermute | solution.py:36
  228.4 200.4 %copy-start = (f32[9000,128]{1,0:T(8,128)}, f32[9000,128]{1,0:T(8,128)S(1)}, u32[]{:S(2)}) copy-start(f32[9000,128]{1,0:T(8,128)S(1)} %add.48) | copy-start | bytes 13824004
  228.4 200.3 %collective-permute-start.2 = (f32[9000,128]{1,0:T(8,128)S(1)}, f32[9000,128]{1,0:T(8,128)S(1)}, u32[]{:S(2)}, u32[]{:S(2)}) collective-permute-start(f32[9000,128]{1,0:T(8,128)S(1)} %add.48), channel_id=1, source_target_pairs={{0,16},{4,20},{8,24},{12,28},{16,0},{20,4},{24,8},{28,12},{1,17},{... | collective-permute-start | bytes 13824008 | tf_op jit(solution)/shard_map/ppermute | solution.py:36
  428.8 2.1 copy-start.3
  439.5 144.1 %all-reduce.11.cloned.1.call-start = ((), (), s32[]{:S(2)}) async-start(), calls=%async_computation.2 | async-start | bytes 1048576 | tf_op jit(solution)/shard_map/psum | solution.py:24
  538.0 443.8 %all-reduce.13.cloned.1.call-start = ((), (), s32[]{:S(2)}) async-start(), calls=%async_computation.3 | async-start | bytes 131072 | tf_op jit(solution)/shard_map/psum | solution.py:42
  618.0 7.8 collective-permute-start.3
  626.3 101.5 %collective-permute-start.4 = (f32[9000,128]{1,0:T(8,128)S(1)}, f32[9000,128]{1,0:T(8,128)S(1)}, u32[]{:S(2)}, u32[]{:S(2)}) collective-permute-start(f32[9000,128]{1,0:T(8,128)S(1)} %add.50), channel_id=1, source_target_pairs={{0,8},{4,12},{8,0},{12,4},{16,24},{20,28},{24,16},{28,20},{1,9},{5... | collective-permute-start | bytes 13824008 | tf_op jit(solution)/shard_map/ppermute | solution.py:36
  728.8 200.4 %copy-start.1 = (f32[9000,128]{1,0:T(8,128)}, f32[9000,128]{1,0:T(8,128)S(1)}, u32[]{:S(2)}) copy-start(f32[9000,128]{1,0:T(8,128)S(1)} %add.51) | copy-start | bytes 13824004
  728.8 200.3 %collective-permute-start.5 = (f32[9000,128]{1,0:T(8,128)S(1)}, f32[9000,128]{1,0:T(8,128)S(1)}, u32[]{:S(2)}, u32[]{:S(2)}) collective-permute-start(f32[9000,128]{1,0:T(8,128)S(1)} %add.51), channel_id=1, source_target_pairs={{0,16},{4,20},{8,24},{12,28},{16,0},{20,4},{24,8},{28,12},{1,17},{... | collective-permute-start | bytes 13824008 | tf_op jit(solution)/shard_map/ppermute | solution.py:36
  929.1 2.1 copy-start.4
  939.9 149.9 %all-reduce.15.cloned.1.call-start = ((), (), s32[]{:S(2)}) async-start(), calls=%async_computation.4 | async-start | bytes 1048576 | tf_op jit(solution)/shard_map/psum | solution.py:24
  1016.7 2.2 copy-start.2
  1044.3 103.0 %all-reduce.17.cloned.1.call-start = ((), (), s32[]{:S(2)}) async-start(), calls=%async_computation.5 | async-start | bytes 131072 | tf_op jit(solution)/shard_map/psum | solution.py:52
Sparse Core Ops, SparseCore 0:
  35.1 48.0 all-reduce.6
  439.6 41.8 all-reduce.8
  538.2 45.3 all-reduce.10
  940.0 41.8 all-reduce.12
  1044.5 45.3 all-reduce.14
  1092.6 54.6 all-reduce.16
